TPU v7x, 16 devices: a 4x2x1 block of a 4x4x8 slice. The times are simulated.
16 devices in a mesh: dp: 4 (over y, z, core), ep: 4 (over x).
Axes of the slice: x: 4, y: 2, z: 1, core: 2. Of those that a mesh axis runs over, the one named last changes fastest.
The devices are a block of a 4x4x8 slice.
Arguments:
- x: bfloat16 [4, 4, 256, 2048], P('dp', 'ep'), parts along dimension 0
- expert: int32 [4, 4, 256, 2], P('dp', 'ep'), parts along dimension 0
- slot: int32 [4, 4, 256, 2], P('dp', 'ep'), parts along dimension 0
- gate: float32 [4, 4, 256, 2], P('dp', 'ep'), parts along dimension 0
- w_gate: bfloat16 [8, 2048, 5632], P('ep')
- w_up: bfloat16 [8, 2048, 5632], P('ep')
- w_down: bfloat16 [8, 5632, 2048], P('ep')
Outputs:
- y: bfloat16 [4, 4, 256, 2048], P('dp', 'ep'), parts along dimension 0
There are 4 independent parts. A program takes and returns all parts, laid end to end along the dimension named above; an argument that names none is the same for every part.
All inputs are finite; a program needn't handle non-finite values.
Results may differ from a plain program's by a relative error of at most 0.009.
Values are sent between devices in bfloat16 or wider.
A program may use at most 768 MiB of HBM per device.

v0:
```python
import jax
import jax.numpy as jnp
from jax import lax
from jax.sharding import NamedSharding, PartitionSpec as P


def einsum(form, a, b):
    return jnp.einsum(form, a.astype(jnp.float32), b.astype(jnp.float32))


def solution(mesh):
    def placed(v, *spec):
        return lax.with_sharding_constraint(v, NamedSharding(mesh, P(*spec)))

    def step(x, expert, slot, gate, w_gate, w_up, w_down):
        experts, (tokens, top) = w_gate.shape[0], expert.shape[2:]
        slots = 5 * tokens * top // (4 * experts)
        to_expert = jax.nn.one_hot(expert, experts, dtype=jnp.bfloat16)
        to_slot = jax.nn.one_hot(slot, slots, dtype=jnp.bfloat16)
        weighted = to_expert * gate[..., None].astype(jnp.bfloat16)
        dispatch = einsum("abtke,abtkc->abtec", to_expert, to_slot).astype(jnp.bfloat16)
        combine = einsum("abtke,abtkc->abtec", weighted, to_slot).astype(jnp.bfloat16)
        z = einsum("abtec,abtd->aebcd", dispatch, x).astype(jnp.bfloat16)
        z = placed(z, "dp", None, "ep", None, None)
        z = placed(z, "dp", "ep", None, None, None)
        h = jax.nn.silu(einsum("aebcd,edf->aebcf", z, w_gate))
        h = (h * einsum("aebcd,edf->aebcf", z, w_up)).astype(jnp.bfloat16)
        out = einsum("aebcf,efd->aebcd", h, w_down).astype(jnp.bfloat16)
        out = placed(out, "dp", "ep", None, None, None)
        out = placed(out, "dp", None, "ep", None, None)
        y = einsum("abtec,aebcd->abtd", combine, out)
        return y.astype(jnp.bfloat16)

    return step
```

profile of v0, /device:TPU:113, one launch (start us, length us, event | category | flops | bytes accessed | tf_op | source)
XLA Modules:
  0.0 159.5 jit_solution(7801215851164015591)
XLA Ops:
  0.0 0.0 copy-start
  0.0 0.9 copy.11
  0.9 0.8 copy.9
  1.7 1.8 %convolution_convert_fusion.1 = bf16[256,8,80]{2,1,0:T(8,128)(2,1)S(1)} fusion(s32[256,2]{1,0:T(8,128)S(1)} %copy.11, s32[256,2]{1,0:T(8,128)S(1)} %copy.9), kind=kOutput, calls=%fused_computation.24 | convolution fusion | flops 864256 | bytes 331776 | tf_op jit(solution)/abtke,abtkc->abtec/dot_general | solution.py:8
  3.5 0.0 copy-done
  3.5 0.9 convolution_convert_fusion
  4.4 36.1 %all-to-all.4 = bf16[1,4,2,1,80,2048]{5,4,2,3,0,1:T(8,128)(2,1)} all-to-all(bf16[1,4,2,1,80,2048]{5,4,2,3,0,1:T(8,128)(2,1)S(1)} %bitcast.120), channel_id=1, replica_groups=mesh['dp'=4,'ep'=4] {'ep'}, dimensions={1} | all-to-all | bytes 5242880 | tf_op jit(solution)/sharding_constraint;jit(solution)/sharding_constraint | solution.py:13
  40.5 27.7 %fusion.4 = f32[2,4,80,5632]{3,2,1,0:T(8,128)} fusion(bf16[2,2048,5632]{2,1,0:T(8,128)(2,1)} %param.4, bf16[1,4,2,1,80,2048]{5,4,2,3,0,1:T(8,128)(2,1)} %all-to-all.4), kind=kOutput, calls=%fused_computation.4 | convolution fusion | flops 14763950080 | bytes 63176704 | tf_op jit(solution)/aebcd,edf->aebcf/dot_general | solution.py:8
  68.1 28.8 %fusion.12.clone.4 = bf16[2,4,80,5632]{3,2,1,0:T(8,128)(2,1)} fusion(bf16[2,2048,5632]{2,1,0:T(8,128)(2,1)} %param.5, f32[2,4,80,5632]{3,2,1,0:T(8,128)} %fusion.4, bf16[1,4,2,1,80,2048]{5,4,2,3,0,1:T(8,128)(2,1)} %all-to-all.4), kind=kOutput, calls=%fused_computation.13.clone.clone.clone.1 | convolution fusion | flops 14785576960 | bytes 70385664 | tf_op jit(solution)/aebcd,edf->aebcf/dot_general | solution.py:8
  96.9 22.4 %fusion.18 = bf16[1,2,4,1,80,2048]{5,4,2,1,3,0:T(8,128)(2,1)S(1)} fusion(bf16[2,5632,2048]{2,1,0:T(8,128)(2,1)} %param.6, bf16[2,4,80,5632]{3,2,1,0:T(8,128)(2,1)} %fusion.12.clone.4), kind=kOutput, calls=%fused_computation.16 | convolution fusion | flops 14765260800 | bytes 55967744 | tf_op jit(solution)/aebcf,efd->aebcd/dot_general | solution.py:8
  119.3 0.0 copy-start.2
  119.3 1.7 %copy.15 = bf16[1,2,4,1,80,2048]{5,4,1,3,0,2:T(8,128)(2,1)} copy(bf16[1,2,4,1,80,2048]{5,4,2,1,3,0:T(8,128)(2,1)S(1)} %fusion.18) | data formatting | bytes 5242880 | tf_op jit(solution)/sharding_constraint;jit(solution)/sharding_constraint | solution.py:13
  121.0 4.6 %all-to-all-start.1 = ((bf16[1,2,4,1,80,2048]{5,4,1,3,0,2:T(8,128)(2,1)}), bf16[1,2,4,1,80,2048]{5,4,1,3,0,2:T(8,128)(2,1)}, u32[]{:S(2)}, u32[]{:S(2)}) async-start(bf16[1,2,4,1,80,2048]{5,4,1,3,0,2:T(8,128)(2,1)} %copy.15), calls=%async_computation.1 | async-start | bytes 5242880 | tf_op jit(solution)/sharding_constraint;jit(solution)/sharding_constraint | solution.py:13
  125.6 0.0 copy-done.2
  125.6 0.0 copy-start.1
  125.7 0.1 copy.10
  125.8 2.2 %convolution_convert_fusion.2 = bf16[256,8,80]{2,1,0:T(8,128)(2,1)S(1)} fusion(s32[256,2]{1,0:T(8,128)S(1)} %copy.11, s32[256,2]{1,0:T(8,128)S(1)} %copy.9, bf16[256,2]{1,0:T(8,128)(2,1)S(1)} %copy.10), kind=kOutput, calls=%fused_computation.25 | convolution fusion | flops 868352 | bytes 332800 | tf_op jit(solution)/abtke,abtkc->abtec/dot_general | solution.py:8
  128.0 27.7 %all-to-all-done.1 = bf16[1,2,4,1,80,2048]{5,4,1,3,0,2:T(8,128)(2,1)} async-done(((bf16[1,2,4,1,80,2048]{5,4,1,3,0,2:T(8,128)(2,1)}), bf16[1,2,4,1,80,2048]{5,4,1,3,0,2:T(8,128)(2,1)}, u32[]{:S(2)}, u32[]{:S(2)}) %all-to-all-start.1) | async-done | bytes 2621472 | tf_op jit(solution)/sharding_constraint;jit(solution)/sharding_constraint | solution.py:13
  155.7 3.8 %fusion.24 = bf16[1,1,256,2048]{3,2,1,0:T(8,128)(2,1)} fusion(bf16[8,80,2048]{2,1,0:T(8,128)(2,1)} %bitcast.25, bf16[256,8,80]{2,1,0:T(8,128)(2,1)S(1)} %convolution_convert_fusion.2), kind=kOutput, calls=%fused_computation.21 | convolution fusion | flops 671612928 | bytes 3997696 | tf_op jit(solution)/abtec,aebcd->abtd/dot_general | solution.py:8
  159.5 0.0 copy-done.1
  (1 shorter events, 0.0 us)
Async XLA Ops:
  0.0 3.5 %copy-start = (bf16[1,1,256,2048]{3,2,1,0:T(8,128)(2,1)S(1)}, bf16[1,1,256,2048]{3,2,1,0:T(8,128)(2,1)}, u32[]{:S(2)}) copy-start(bf16[1,1,256,2048]{3,2,1,0:T(8,128)(2,1)} %param.3) | copy-start | bytes 3145732
  119.3 6.3 %copy-start.2 = (f32[1,1,256,2]{2,3,1,0:T(2,128)S(1)}, f32[1,1,256,2]{2,3,1,0:T(2,128)}, u32[]{:S(2)}) copy-start(f32[1,1,256,2]{2,3,1,0:T(2,128)} %param.1) | copy-start | bytes 6148
  121.0 34.7 %all-to-all-start.1 = ((bf16[1,2,4,1,80,2048]{5,4,1,3,0,2:T(8,128)(2,1)}), bf16[1,2,4,1,80,2048]{5,4,1,3,0,2:T(8,128)(2,1)}, u32[]{:S(2)}, u32[]{:S(2)}) async-start(bf16[1,2,4,1,80,2048]{5,4,1,3,0,2:T(8,128)(2,1)} %copy.15), calls=%async_computation.1 | async-start | bytes 5242880 | tf_op jit(solution)/sharding_constraint;jit(solution)/sharding_constraint | solution.py:13
  125.6 33.8 %copy-start.1 = (bf16[1,1,256,2048]{3,2,1,0:T(8,128)(2,1)S(1)}, bf16[1,1,256,2048]{3,2,1,0:T(8,128)(2,1)}, u32[]{:S(2)}) copy-start(bf16[1,1,256,2048]{3,2,1,0:T(8,128)(2,1)} %param.3) | copy-start | bytes 3145732
where the time goes:
time: 162 us; the launch traced here: 159 us
  matrix products  87.4 us (54%)
  blocking collectives  36.1 us (22%)
  waiting for transfers between devices  27.7 us (17%)
  starting transfers between devices  4.64 us (3%)
  local copies, waits for them, and re-layouts  3.56 us (2%)
    dot_general x7, matrix products, einsum(): return jnp.einsum(form, a.astype(jnp.float32), b.astype(jnp.float32))  87.4 us
    another operation x1, blocking collectives, placed(): return lax.with_sharding_constraint(v, NamedSharding(mesh, P(*spec)))  36.1 us
    another operation x1, waiting for transfers between devices, placed(): return lax.with_sharding_constraint(v, NamedSharding(mesh, P(*spec)))  27.7 us
    another operation x1, starting transfers between devices, placed(): return lax.with_sharding_constraint(v, NamedSharding(mesh, P(*spec)))  4.64 us
  transfers between devices with their start and end apart: 1, of which 1 were waited for; matrix products, arithmetic and copies ran while one was open for 1% of the time, Pallas kernels for 0%

commit v1 on v0

v1 whole, which is shorter than its diff:
```python
import functools

import jax
import jax.numpy as jnp
from jax import lax
from jax.experimental import pallas as pl
from jax.experimental.pallas import tpu as pltpu
from jax.sharding import PartitionSpec as P

MESH = pl.DeviceIdType.MESH
PLACE = {0: 0, 2: 1, 1: 2, 3: 3}
DISTANCE = {place: k for k, place in PLACE.items()}
RING = 7
UNIT = 512
TILE = 512
F32 = jnp.float32
BF16 = jnp.bfloat16


def dot(a, b):
    return jnp.dot(a, b, preferred_element_type=F32)


def kernel(slots, info_ref, x_ref, wg, wu, wd, y_ref, zs, zr, h, os, orv, w1, w2, comb,
           w1_sem, w2_sem, zs_sem, zr_sem, os_sem, or_sem, ns_sem, nr_sem, ls_sem, lr_sem):
    tokens, d = x_ref.shape
    ff = h.shape[1]
    pair = 2 * slots
    units, tiles = ff // UNIT, d // TILE
    n = 4
    me, group = lax.axis_index("ep"), lax.axis_index("dp")
    core = lax.rem(group, 2)
    base = group - core

    def device(k, c):
        return {"ep": lax.rem(me + k, n), "dp": base + c}

    def partner():
        return {"ep": me, "dp": base + 1 - core}

    barrier = pltpu.get_barrier_semaphore()
    pl.semaphore_signal(barrier, inc=1, device_id=partner(), device_id_type=MESH)
    for k in range(1, n):
        for c in range(2):
            pl.semaphore_signal(barrier, inc=1, device_id=device(k, c), device_id_type=MESH)

    def w1_copies(unit, slot):
        columns = pl.ds(pl.multiple_of(unit * UNIT, UNIT), UNIT)
        return [
            pltpu.make_async_copy(w.at[core, :, columns], w1.at[slot, i], w1_sem.at[slot, i])
            for i, w in enumerate((wg, wu))
        ]

    def w2_copy(tile, slot):
        columns = pl.ds(pl.multiple_of(tile * TILE, TILE), TILE)
        return pltpu.make_async_copy(wd.at[core, :, columns], w2.at[slot], w2_sem.at[slot])

    def unit_of(turn, p):
        return lax.rem(p + (units - RING) * turn, units)

    def slot_of(turn, p):
        return lax.rem(units * turn + p, RING)

    for p in range(RING):
        for copy in w1_copies(p, p):
            copy.start()

    info = info_ref[...]
    across = jnp.concatenate([info, jnp.zeros((128 - info.shape[0], tokens), F32)], axis=0).T

    def owner(place):
        return (lax.rem(me + DISTANCE[place], n) * pair).astype(F32)

    def dispatch(place):
        row = lax.broadcasted_iota(jnp.int32, (pair, tokens), 0).astype(F32) + owner(place)
        pick = (info[0:1] == row) | (info[1:2] == row)
        pick = jnp.where(pick, 1.0, 0.0).astype(BF16)
        for t in range(d // 512):
            columns = slice(t * 512, (t + 1) * 512)
            zs[place * pair:(place + 1) * pair, columns] = dot(pick, x_ref[:, columns]).astype(BF16)

    def z_copy(place, c):
        k = DISTANCE[place]
        there = PLACE[(n - k) % n]
        return pltpu.make_async_remote_copy(
            src_ref=zs.at[pl.ds(place * pair + c * slots, slots)],
            dst_ref=zr.at[pl.ds(pl.multiple_of(there * pair + core * slots, 16), slots)],
            send_sem=zs_sem.at[place * 2 + c],
            recv_sem=zr_sem.at[there * 2 + core],
            device_id=device(k, c) if k else partner(),
            device_id_type=MESH,
        )

    def arrived(ref, sem):
        pltpu.make_async_remote_copy(
            src_ref=ref, dst_ref=ref, send_sem=sem, recv_sem=sem, device_id=partner(), device_id_type=MESH
        ).wait_recv()

    def z_arrived(place, c):
        arrived(zr.at[pl.ds(place * pair + c * slots, slots)], zr_sem.at[place * 2 + c])

    own = pl.ds(pl.multiple_of(core * slots, 16), slots)
    other = 1 - core
    dispatch(1)
    dispatch(0)
    pl.semaphore_wait(barrier, 2 * n - 1)
    for c in range(2):
        z_copy(1, c).start()
    to_partner = pltpu.make_async_remote_copy(
        src_ref=zs.at[pl.ds(pl.multiple_of(other * slots, 16), slots)],
        dst_ref=zr.at[own],
        send_sem=zs_sem.at[0],
        recv_sem=zr_sem.at[0],
        device_id=partner(),
        device_id_type=MESH,
    )
    to_partner.start()
    zr[own, :] = zs[own, :]
    dispatch(2)
    dispatch(3)
    for place in range(n):
        column = lax.broadcasted_iota(jnp.int32, (tokens, pair), 1).astype(F32) + owner(place)
        weight = jnp.where(across[:, 0:1] == column, across[:, 2:3], 0.0)
        weight = weight + jnp.where(across[:, 1:2] == column, across[:, 3:4], 0.0)
        comb[place] = weight.astype(BF16)
    to_partner.wait_recv()

    def project(turn, p, first, rows):
        slot, unit = slot_of(turn, p), unit_of(turn, p)
        z = zr[first:first + rows, :]
        a = dot(z, w1[slot, 0])
        b = dot(z, w1[slot, 1])
        columns = pl.ds(pl.multiple_of(unit * UNIT, UNIT), UNIT)
        h[first:first + rows, columns] = (a * jax.nn.sigmoid(a) * b).astype(BF16)

    def up_pass(turn, first, rows, extra=None):
        def step(p, _):
            def arrive():
                for copy in w1_copies(unit_of(turn, p), slot_of(turn, p)):
                    copy.wait()

            if turn == 0:
                arrive()
            else:
                pl.when(p >= RING)(arrive)
            project(turn, p, first, rows)

            @pl.when(p < units - RING)
            def _():
                for copy in w1_copies(unit_of(turn, p + RING), slot_of(turn, p)):
                    copy.start()

            if extra is not None:
                extra(p)
            return 0

        lax.fori_loop(0, units, step, 0)

    def first_extra(p):
        @pl.when(p == units - RING)
        def _():
            for tile in range(2):
                w2_copy(tile, tile).start()

        @pl.when(p == SEND_N)
        def _():
            for place in (2, 3):
                for c in range(2):
                    z_copy(place, c).start()

    up_pass(0, 0, pair, first_extra)
    for c in range(2):
        z_arrived(1, c)
    up_pass(1, pair, pair)

    def far_step(i, _):
        slot = lax.rem(i, 2)
        w2_copy(i, slot).wait()
        os[i, pair:2 * pair, :] = dot(h[pair:2 * pair, :], w2[slot]).astype(BF16)

        @pl.when(i < 2)
        def _():
            w2_copy(i + 2, slot).start()

        return 0

    lax.fori_loop(0, tiles, far_step, 0)

    for place in (2, 3):
        for c in range(2):
            z_arrived(place, c)

    def far_copy(c):
        return pltpu.make_async_remote_copy(
            src_ref=os.at[:, pl.ds(pair + c * slots, slots), :],
            dst_ref=orv.at[:, pl.ds(pl.multiple_of(pair + core * slots, 16), slots), :],
            send_sem=os_sem.at[c],
            recv_sem=or_sem.at[core],
            device_id=device(2, c),
            device_id_type=MESH,
        )

    for c in range(2):
        far_copy(c).start()

    up_pass(2, 2 * pair, 2 * pair)

    def near_copy(tile, place, c):
        k = DISTANCE[place]
        there = PLACE[(n - k) % n]
        return pltpu.make_async_remote_copy(
            src_ref=os.at[tile, pl.ds(place * pair + c * slots, slots), :],
            dst_ref=orv.at[tile, pl.ds(pl.multiple_of(there * pair + core * slots, 16), slots), :],
            send_sem=ns_sem.at[tile, (place - 2) * 2 + c],
            recv_sem=nr_sem.at[tile, (there - 2) * 2 + core],
            device_id=device(k, c),
            device_id_type=MESH,
        )

    def partner_copy(tile):
        return pltpu.make_async_remote_copy(
            src_ref=os.at[tile, pl.ds(pl.multiple_of(other * slots, 16), slots), :],
            dst_ref=orv.at[tile, own, :],
            send_sem=ls_sem.at[tile],
            recv_sem=lr_sem.at[tile],
            device_id=partner(),
            device_id_type=MESH,
        )

    def near_step(i, _):
        tile, slot = lax.rem(i + 2, tiles), lax.rem(i, 2)

        @pl.when(i >= 2)
        def _():
            w2_copy(tile, slot).wait()

        os[tile, 2 * pair:4 * pair, :] = dot(h[2 * pair:4 * pair, :], w2[slot]).astype(BF16)
        for place in (2, 3):
            for c in range(2):
                near_copy(tile, place, c).start()
        os[tile, 0:pair, :] = dot(h[0:pair, :], w2[slot]).astype(BF16)
        partner_copy(tile).start()
        orv[tile, own, :] = os[tile, own, :]

        @pl.when(i < 2)
        def _():
            w2_copy(i, slot).start()

        return 0

    lax.fori_loop(0, tiles, near_step, 0)

    for c in range(2):
        arrived(orv.at[:, pl.ds(pair + c * slots, slots), :], or_sem.at[c])
    for i in range(tiles):
        tile = (i + 2) % tiles
        for place in (2, 3):
            for c in range(2):
                rows = pl.ds(place * pair + c * slots, slots)
                arrived(orv.at[tile, rows, :], nr_sem.at[tile, (place - 2) * 2 + c])
        partner_copy(tile).wait_recv()
        total = dot(comb[0], orv[tile, 0:pair, :])
        for place in range(1, n):
            total = total + dot(comb[place], orv[tile, place * pair:(place + 1) * pair, :])
        y_ref[:, tile * TILE:(tile + 1) * TILE] = total.astype(BF16)

    to_partner.wait_send()
    for c in range(2):
        for place in range(1, n):
            z_copy(place, c).wait_send()
        far_copy(c).wait_send()
    for tile in range(tiles):
        partner_copy(tile).wait_send()
        for place in (2, 3):
            for c in range(2):
                near_copy(tile, place, c).wait_send()


SEND_N = 8


def solution(mesh):
    def body(x, expert, slot, gate, w_gate, w_up, w_down):
        tokens, d = x.shape[2:]
        top = expert.shape[3]
        held, _, ff = w_gate.shape
        experts = held * mesh.shape["ep"]
        slots = 5 * tokens * top // (4 * experts)
        rows = experts * slots
        code = jnp.where(slot < slots, expert * slots + slot, -1)[0, 0].T.astype(F32)
        weight = gate.astype(BF16)[0, 0].T.astype(F32)
        info = jnp.concatenate([code, weight, jnp.zeros((4, tokens), F32)], axis=0)
        vmem = pl.BlockSpec(memory_space=pltpu.VMEM)
        hbm = pl.BlockSpec(memory_space=pltpu.HBM)
        tiles = d // TILE
        dma = pltpu.SemaphoreType.DMA
        y = pl.pallas_call(
            functools.partial(kernel, slots),
            name="moe",
            out_shape=jax.ShapeDtypeStruct((tokens, d), BF16),
            in_specs=[vmem, vmem, hbm, hbm, hbm],
            out_specs=vmem,
            scratch_shapes=[
                pltpu.VMEM((rows, d), BF16),
                pltpu.VMEM((rows, d), BF16),
                pltpu.VMEM((rows, ff), BF16),
                pltpu.VMEM((tiles, rows, TILE), BF16),
                pltpu.VMEM((tiles, rows, TILE), BF16),
                pltpu.VMEM((RING, 2, d, UNIT), BF16),
                pltpu.VMEM((2, ff, TILE), BF16),
                pltpu.VMEM((4, tokens, 2 * slots), BF16),
                dma((RING, 2)),
                dma((2,)),
                dma((8,)),
                dma((8,)),
                dma((2,)),
                dma((2,)),
                dma((tiles, 4)),
                dma((tiles, 4)),
                dma((tiles,)),
                dma((tiles,)),
            ],
            compiler_params=pltpu.CompilerParams(
                collective_id=0, has_side_effects=True, vmem_limit_bytes=67_000_000
            ),
        )(info, x[0, 0], w_gate, w_up, w_down)
        return y[None, None]

    part = P("dp", "ep")
    weights = P("ep")
    return jax.shard_map(
        body, mesh=mesh, in_specs=(part, part, part, part, weights, weights, weights), out_specs=part, check_vma=False
    )
```

time: 162 us -> 78.9 us (0.49); the launches traced: 159 us -> 78.7 us
  matrix products: 87.4 us -> 0 us
  Pallas kernels: 0 us -> 74.3 us
  blocking collectives: 36.1 us -> 0 us
  waiting for transfers between devices: 27.7 us -> 0 us
  starting transfers between devices: 4.64 us -> 0 us
  other arithmetic: 0.01 us -> 2.05 us
    dot_general x7 -> x0, matrix products: 87.4 us -> none  [einsum(): return jnp.einsum(form, a.astype(jnp.float32), b.astype(jnp.float32))]
    pallas_call x0 -> x1, Pallas kernels: none -> 74.3 us  [body(): pl.pallas_call(functools.partial(kernel, slots), name='moe', out_shape=ja...]
    another operation x1 -> x0, blocking collectives: 36.1 us -> none  [placed(): return lax.with_sharding_constraint(v, NamedSharding(mesh, P(*spec)))]
    another operation x1 -> x0, waiting for transfers between devices: 27.7 us -> none  [placed(): return lax.with_sharding_constraint(v, NamedSharding(mesh, P(*spec)))]
    another operation x1 -> x0, starting transfers between devices: 4.64 us -> none  [placed(): return lax.with_sharding_constraint(v, NamedSharding(mesh, P(*spec)))]
    another operation x1 -> x0, local copies, waits for them, and re-layouts: 1.68 us -> none  [placed(): return lax.with_sharding_constraint(v, NamedSharding(mesh, P(*spec)))]
  transfers between devices with their start and end apart: 1 -> 0, of which waited for: 1 -> 0; matrix products, arithmetic and copies ran while one was open for 1% -> 0% of each run, Pallas kernels for 0% -> 0%
where the time goes in v1:
time: 78.9 us; the launch traced here: 78.7 us
  Pallas kernels  74.3 us (94%)
  local copies, waits for them, and re-layouts  2.38 us (3%)
  other arithmetic  2.05 us (3%)
    pallas_call x1, Pallas kernels, body(): pl.pallas_call(functools.partial(kernel, slots), name='moe', out_shape=ja...  74.3 us
    unnamed x1, local copies, waits for them, and re-layouts  2.3 us

profile of v1, /device:TPU:113, one launch (start us, length us, event | category | flops | bytes accessed | tf_op | source)
XLA Modules:
  0.0 78.7 jit_solution(14077041402315137557)
XLA Ops:
  0.0 0.1 pad.2.clone
  0.1 0.7 fusion.1
  0.8 0.7 convert_bitcast_fusion
  1.5 0.7 maximum_maximum_fusion.info_ref
  2.1 74.3 %moe.1 = bf16[256,2048]{1,0:T(8,128)(2,1)} custom-call(f32[8,256]{1,0:T(8,128)} %maximum_maximum_fusion.info_ref, bf16[256,2048]{1,0:T(8,128)(2,1)} %bitcast.12, bf16[2,2048,5632]{2,1,0:T(8,128)(2,1)} %wg.1, bf16[2,2048,5632]{2,1,0:T(8,128)(2,1)} %wu.1, bf16[2,5632,2048]{2,1,0:T(8,128)(2,1)} %wd.1), custom_call_target="tpu_custom_call" | custom-call | tf_op jit(solution)/shard_map/moe/pallas_call | solution.py:297
  76.4 2.3 %copy.9 = bf16[1,1,256,2048]{3,2,1,0:T(8,128)(2,1)} copy(bf16[1,1,256,2048]{3,2,1,0:T(8,128)(2,1)} %bitcast.11) | data formatting | bytes 2097152
  (1 shorter events, 0.0 us)

commit v2 on v0

v2 whole, which is shorter than its diff:
```python
import functools

import jax
import jax.numpy as jnp
from jax import lax
from jax.experimental import pallas as pl
from jax.experimental.pallas import tpu as pltpu
from jax.sharding import PartitionSpec as P

MESH = pl.DeviceIdType.MESH
MEMBERS = 4
BLOCKS = [(0, 0), (0, 1), (1, 0), (3, 0), (2, 0), (2, 1), (1, 1), (3, 1)]
L, N1, O, N2 = range(4)
RING = 7
UNIT = 512
TILE = 512
F32 = jnp.float32
BF16 = jnp.bfloat16


def there(block):
    k, rel = BLOCKS[block]
    return BLOCKS.index(((MEMBERS - k) % MEMBERS, rel))


def dot(a, b):
    return jnp.dot(a, b, preferred_element_type=F32)


def kernel(slots, expert, slot, gate, x_hbm, wg, wu, wd, y_ref, x, zs, zr, h, os, orv, w1, w2, comb,
           x_sem, w1_sem, w2_sem, zs_sem, zr_sem, os_sem, or_sem):
    tokens, d = x.shape
    ff = h.shape[1]
    pair = 2 * slots
    units, tiles = ff // UNIT, d // TILE
    me, group = lax.axis_index("ep"), lax.axis_index("dp")
    core = lax.rem(group, 2)
    base = group - core
    cores = (core, 1 - core)

    def device(block):
        k, rel = BLOCKS[block]
        return {"ep": lax.rem(me + k, MEMBERS), "dp": base + cores[rel]}

    def first_code(block):
        k, rel = BLOCKS[block]
        return (2 * lax.rem(me + k, MEMBERS) + cores[rel]) * slots

    def rows(block):
        return pl.ds(block * slots, slots)

    def chunk(c):
        return slice(c * pair, (c + 1) * pair)

    def columns(t, width):
        return pl.ds(pl.multiple_of(t * width, width), width)

    def x_copy(t):
        return pltpu.make_async_copy(x_hbm.at[:, columns(t, TILE)], x.at[:, columns(t, TILE)], x_sem.at[t])

    def w1_start(unit, at):
        for i, w in enumerate((wg, wu)):
            pltpu.make_async_copy(w.at[core, :, columns(unit, UNIT)], w1.at[at, i], w1_sem.at[at, i]).start()

    def w1_wait(at):
        for i in range(2):
            pltpu.make_async_copy(w1.at[at, i], w1.at[at, i], w1_sem.at[at, i]).wait()

    def w2_copy(tile, at):
        return pltpu.make_async_copy(wd.at[core, :, columns(tile, TILE)], w2.at[at], w2_sem.at[at])

    def z_copy(block):
        return pltpu.make_async_remote_copy(
            src_ref=zs.at[rows(block)],
            dst_ref=zr.at[rows(there(block))],
            send_sem=zs_sem.at[block],
            recv_sem=zr_sem.at[there(block)],
            device_id=device(block),
            device_id_type=MESH,
        )

    def o_copy(tile, block):
        return pltpu.make_async_remote_copy(
            src_ref=os.at[tile, rows(block)],
            dst_ref=orv.at[tile, rows(there(block))],
            send_sem=os_sem.at[tile, block],
            recv_sem=or_sem.at[tile, there(block)],
            device_id=device(block),
            device_id_type=MESH,
        )

    def z_arrived(block):
        ref, sem = zr.at[rows(block)], zr_sem.at[block]
        pltpu.make_async_copy(ref, ref, sem).wait()

    def o_arrived(tile, block):
        ref, sem = orv.at[tile, rows(block)], or_sem.at[tile, block]
        pltpu.make_async_copy(ref, ref, sem).wait()

    for t in range(tiles):
        x_copy(t).start()
    barrier = pltpu.get_barrier_semaphore()
    for block in range(1, len(BLOCKS)):
        pl.semaphore_signal(barrier, inc=1, device_id=device(block), device_id_type=MESH)
    for p in range(RING):
        w1_start(p, p)

    code = jnp.where(slot[...] < slots, expert[...] * slots + slot[...], -1)

    def bases(index, c):
        return index + jnp.where(index < slots, first_code(2 * c), first_code(2 * c + 1) - slots)

    def dispatch(c):
        row = bases(lax.broadcasted_iota(jnp.int32, (pair, tokens), 0), c)
        pick = (code[0:1] == row) | (code[1:2] == row)
        pick = jnp.where(pick, 1.0, 0.0).astype(BF16)
        for t in range(tiles):
            if c == N1:
                x_copy(t).wait()
            at = slice(t * TILE, (t + 1) * TILE)
            z = dot(pick, x[:, at]).astype(BF16)
            if c == L:
                zr[0:slots, at] = z[0:slots]
                zs[slots:pair, at] = z[slots:pair]
            else:
                zs[chunk(c), at] = z

    dispatch(N1)
    dispatch(L)
    pl.semaphore_wait(barrier, len(BLOCKS) - 1)
    z_copy(2 * N1).start()
    z_copy(2 * N1 + 1).start()
    z_copy(2 * L + 1).start()
    dispatch(O)
    z_copy(2 * O).start()
    z_copy(2 * O + 1).start()
    dispatch(N2)

    table = jnp.concatenate([code.astype(F32), gate[...], jnp.zeros((124, tokens), F32)], axis=0).T
    for c in range(4):
        column = bases(lax.broadcasted_iota(jnp.int32, (tokens, pair), 1), c).astype(F32)
        weight = jnp.where(table[:, 0:1] == column, table[:, 2:3], 0.0)
        weight = weight + jnp.where(table[:, 1:2] == column, table[:, 3:4], 0.0)
        comb[c] = weight.astype(BF16)

    fresh = units - RING

    def up_pass(turn, c, extra=None):
        def place(p):
            return lax.rem(units * turn + p, RING)

        def unit_of(p):
            return lax.rem(p + fresh * turn, units)

        def project(p):
            at = place(p)
            z = zr[chunk(c), :]
            a = dot(z, w1[at, 0])
            b = dot(z, w1[at, 1])
            h[chunk(c), columns(unit_of(p), UNIT)] = (a * jax.nn.sigmoid(a) * b).astype(BF16)

        def step(i, _):
            for p in (2 * i, 2 * i + 1):
                if turn == 0:
                    w1_wait(place(p))
                else:
                    pl.when(p >= RING)(functools.partial(w1_wait, place(p)))
            for p in (2 * i, 2 * i + 1):
                project(p)

            @pl.when(i < fresh // 2)
            def _():
                for p in (2 * i, 2 * i + 1):
                    w1_start(unit_of(p + RING), place(p))

            if extra is not None:
                extra(i)
            return 0

        lax.fori_loop(0, units // 2, step, 0)
        w1_wait(place(units - 1))
        project(units - 1)

    def down_pass(turn, c):
        def step(i, _):
            tile, at = lax.rem(i + 2 * turn, tiles), lax.rem(i, 2)
            if turn == 0:
                w2_copy(tile, at).wait()
            else:
                pl.when(i >= 2)(lambda: w2_copy(tile, at).wait())
            out = dot(h[chunk(c), :], w2[at]).astype(BF16)
            if c == L:
                orv[tile, 0:slots, :] = out[0:slots]
                os[tile, slots:pair, :] = out[slots:pair]
            else:
                os[tile, chunk(c), :] = out
                o_copy(tile, 2 * c).start()
            o_copy(tile, 2 * c + 1).start()

            @pl.when(i < 2)
            def _():
                w2_copy(lax.rem(i + 2 + 2 * turn, tiles), at).start()

            return 0

        lax.fori_loop(0, tiles, step, 0)

    def load_down(i):
        @pl.when(i == fresh // 2)
        def _():
            for tile in range(2):
                w2_copy(tile, tile).start()

    def send_n2(i):
        @pl.when(i == SEND_N2)
        def _():
            z_copy(2 * N2).start()
            z_copy(2 * N2 + 1).start()

    def wait_z(c):
        z_arrived(2 * c)
        z_arrived(2 * c + 1)

    z_arrived(2 * L + 1)
    up_pass(0, L, load_down)
    wait_z(N1)
    up_pass(1, N1, send_n2)
    down_pass(0, N1)
    wait_z(O)
    up_pass(2, O)
    down_pass(1, O)
    wait_z(N2)
    up_pass(3, N2)
    down_pass(2, N2)
    down_pass(3, L)

    for tile in range(tiles):
        for block in range(1, len(BLOCKS)):
            o_arrived(tile, block)
        total = dot(comb[0], orv[tile, chunk(0), :])
        for c in range(1, 4):
            total = total + dot(comb[c], orv[tile, chunk(c), :])
        y_ref[:, tile * TILE:(tile + 1) * TILE] = total.astype(BF16)

    for block in range(1, len(BLOCKS)):
        z_copy(block).wait_send()
        for tile in range(tiles):
            o_copy(tile, block).wait_send()


SEND_N2 = 3


def solution(mesh):
    def body(x, expert, slot, gate, w_gate, w_up, w_down):
        tokens, d = x.shape[2:]
        top = expert.shape[3]
        held, _, ff = w_gate.shape
        experts = held * mesh.shape["ep"]
        slots = 5 * tokens * top // (4 * experts)
        rows = experts * slots
        vmem = pl.BlockSpec(memory_space=pltpu.VMEM)
        hbm = pl.BlockSpec(memory_space=pltpu.HBM)
        tiles = d // TILE
        dma = pltpu.SemaphoreType.DMA
        y = pl.pallas_call(
            functools.partial(kernel, slots),
            name="moe",
            out_shape=OUT((tokens, d), BF16),
            in_specs=[vmem, vmem, vmem, hbm, hbm, hbm, hbm],
            out_specs=vmem,
            scratch_shapes=[
                pltpu.VMEM((tokens, d), BF16),
                pltpu.VMEM((rows, d), BF16),
                pltpu.VMEM((rows, d), BF16),
                pltpu.VMEM((rows, ff), BF16),
                pltpu.VMEM((tiles, rows, TILE), BF16),
                pltpu.VMEM((tiles, rows, TILE), BF16),
                pltpu.VMEM((RING, 2, d, UNIT), BF16),
                pltpu.VMEM((2, ff, TILE), BF16),
                pltpu.VMEM((4, tokens, 2 * slots), BF16),
                dma((tiles,)),
                dma((RING, 2)),
                dma((2,)),
                dma((8,)),
                dma((8,)),
                dma((tiles, 8)),
                dma((tiles, 8)),
            ],
            compiler_params=pltpu.CompilerParams(
                collective_id=0, has_side_effects=True, vmem_limit_bytes=LIMIT
            ),
        )(expert[0, 0].T, slot[0, 0].T, gate[0, 0].T, x[0, 0], w_gate, w_up, w_down)
        return y[None, None]

    part = P("dp", "ep")
    weights = P("ep")
    return jax.shard_map(
        body, mesh=mesh, in_specs=(part, part, part, part, weights, weights, weights), out_specs=part, check_vma=False
    )


OUT = pltpu.VMEM
LIMIT = 65_800_000
```

time: 162 us -> 75.3 us (0.46); the launches traced: 159 us -> 75.1 us
  matrix products: 87.4 us -> 0 us
  Pallas kernels: 0 us -> 74.1 us
  blocking collectives: 36.1 us -> 0 us
  waiting for transfers between devices: 27.7 us -> 0 us
  starting transfers between devices: 4.64 us -> 0 us
  local copies, waits for them, and re-layouts: 3.56 us -> 0.97 us
    dot_general x7 -> x0, matrix products: 87.4 us -> none  [einsum(): return jnp.einsum(form, a.astype(jnp.float32), b.astype(jnp.float32))]
    pallas_call x0 -> x1, Pallas kernels: none -> 74.1 us  [body(): pl.pallas_call(functools.partial(kernel, slots), name='moe', out_shape=OU...]
    another operation x1 -> x0, blocking collectives: 36.1 us -> none  [placed(): return lax.with_sharding_constraint(v, NamedSharding(mesh, P(*spec)))]
    another operation x1 -> x0, waiting for transfers between devices: 27.7 us -> none  [placed(): return lax.with_sharding_constraint(v, NamedSharding(mesh, P(*spec)))]
    another operation x1 -> x0, starting transfers between devices: 4.64 us -> none  [placed(): return lax.with_sharding_constraint(v, NamedSharding(mesh, P(*spec)))]
    another operation x1 -> x0, local copies, waits for them, and re-layouts: 1.68 us -> none  [placed(): return lax.with_sharding_constraint(v, NamedSharding(mesh, P(*spec)))]
  transfers between devices with their start and end apart: 1 -> 0, of which waited for: 1 -> 0; matrix products, arithmetic and copies ran while one was open for 1% -> 0% of each run, Pallas kernels for 0% -> 0%
where the time goes in v2:
time: 75.3 us; the launch traced here: 75.1 us
  Pallas kernels  74.1 us (98%)
  local copies, waits for them, and re-layouts  0.97 us (1%)
    pallas_call x1, Pallas kernels, body(): pl.pallas_call(functools.partial(kernel, slots), name='moe', out_shape=OU...  74.1 us

profile of v2, /device:TPU:113, one launch (start us, length us, event | category | flops | bytes accessed | tf_op | source)
XLA Modules:
  0.0 75.1 jit_solution(614325274917053962)
XLA Ops:
  0.0 74.1 %moe.1 = bf16[256,2048]{1,0:T(8,128)(2,1)S(1)} custom-call(s32[2,256]{1,0:T(2,128)} %bitcast.13, s32[2,256]{1,0:T(2,128)} %bitcast.14, f32[2,256]{1,0:T(2,128)} %bitcast.15, bf16[256,2048]{1,0:T(8,128)(2,1)} %bitcast.12, bf16[2,2048,5632]{2,1,0:T(8,128)(2,1)} %wg.1, bf16[2,2048,5632]{2,1,0:T(8,128)(2,1)} %wu.1, bf16[2,5632,2048]{2,1,0:T(8,128)(2,1)} %wd.1), custom_call_target="tpu_custom_call" | custom-call | tf_op jit(solution)/shard_map/moe/pallas_call | solution.py:266
  74.1 1.0 %copy.9 = bf16[1,1,256,2048]{3,2,1,0:T(8,128)(2,1)} copy(bf16[1,1,256,2048]{3,2,1,0:T(8,128)(2,1)S(1)} %bitcast.11) | data formatting | bytes 2097152

commit v3 on v2

v3 whole, which is shorter than its diff:
```python
import functools

import jax
import jax.numpy as jnp
from jax import lax
from jax.experimental import pallas as pl
from jax.experimental.pallas import tpu as pltpu
from jax.sharding import PartitionSpec as P

MESH = pl.DeviceIdType.MESH
MEMBERS = 4
BLOCKS = [(0, 0), (0, 1), (1, 0), (3, 0), (2, 0), (2, 1), (1, 1), (3, 1)]
L, N1, O, N2 = range(4)
RING = 7
UNIT = 512
TILE = 512
F32 = jnp.float32
BF16 = jnp.bfloat16


def there(block):
    k, rel = BLOCKS[block]
    return BLOCKS.index(((MEMBERS - k) % MEMBERS, rel))


def dot(a, b):
    return jnp.dot(a, b, preferred_element_type=F32)


def kernel(slots, expert, slot, gate, x_hbm, wg, wu, wd, y_ref, zs, zr, h, orv, w1, w2,
           x_sem, w1_sem, w2_sem, zs_sem, zr_sem, os_sem, or_sem):
    tokens, d = y_ref.shape
    ff = h.shape[1]
    pair = 2 * slots
    units, tiles = ff // UNIT, d // TILE
    me, group = lax.axis_index("ep"), lax.axis_index("dp")
    core = lax.rem(group, 2)
    base = group - core
    cores = (core, 1 - core)

    def device(block):
        k, rel = BLOCKS[block]
        return {"ep": lax.rem(me + k, MEMBERS), "dp": base + cores[rel]}

    def first_code(block):
        k, rel = BLOCKS[block]
        return (2 * lax.rem(me + k, MEMBERS) + cores[rel]) * slots

    def rows(block):
        return pl.ds(block * slots, slots)

    def chunk(c):
        return slice(c * pair, (c + 1) * pair)

    def columns(t, width):
        return pl.ds(pl.multiple_of(t * width, width), width)

    def sent(c):
        return slice(c * pair - slots, (c + 1) * pair - slots)

    def hidden(c):
        return slice(0, pair) if c == L else slice(pair, 2 * pair)

    def x_copy(t):
        return pltpu.make_async_copy(x_hbm.at[:, columns(t, TILE)], y_ref.at[:, columns(t, TILE)], x_sem.at[t])

    def w1_start(unit, at):
        for i, w in enumerate((wg, wu)):
            pltpu.make_async_copy(w.at[core, :, columns(unit, UNIT)], w1.at[at, i], w1_sem.at[at, i]).start()

    def w1_wait(at):
        for i in range(2):
            pltpu.make_async_copy(w1.at[at, i], w1.at[at, i], w1_sem.at[at, i]).wait()

    def w2_copy(tile):
        return pltpu.make_async_copy(wd.at[core, :, columns(tile, TILE)], w2.at[tile], w2_sem.at[tile])

    def z_copy(block):
        return pltpu.make_async_remote_copy(
            src_ref=zs.at[rows(block - 1)],
            dst_ref=zr.at[rows(there(block))],
            send_sem=zs_sem.at[block],
            recv_sem=zr_sem.at[there(block)],
            device_id=device(block),
            device_id_type=MESH,
        )

    def o_copy(tile, block):
        return pltpu.make_async_remote_copy(
            src_ref=zs.at[rows(block - 1), columns(tile, TILE)],
            dst_ref=orv.at[tile, rows(there(block))],
            send_sem=os_sem.at[tile, block],
            recv_sem=or_sem.at[tile, there(block)],
            device_id=device(block),
            device_id_type=MESH,
        )

    def z_arrived(block):
        ref, sem = zr.at[rows(block)], zr_sem.at[block]
        pltpu.make_async_copy(ref, ref, sem).wait()

    def o_arrived(tile, block):
        ref, sem = orv.at[tile, rows(block)], or_sem.at[tile, block]
        pltpu.make_async_copy(ref, ref, sem).wait()

    for t in range(tiles):
        x_copy(t).start()
    barrier = pltpu.get_barrier_semaphore()
    for block in range(1, len(BLOCKS)):
        pl.semaphore_signal(barrier, inc=1, device_id=device(block), device_id_type=MESH)
    for p in range(RING):
        w1_start(p, p)

    code = jnp.where(slot[...] < slots, expert[...] * slots + slot[...], -1)

    def bases(index, c):
        return index + jnp.where(index < slots, first_code(2 * c), first_code(2 * c + 1) - slots)

    def dispatch(c):
        row = bases(lax.broadcasted_iota(jnp.int32, (pair, tokens), 0), c)
        pick = (code[0:1] == row) | (code[1:2] == row)
        pick = jnp.where(pick, 1.0, 0.0).astype(BF16)
        for t in range(tiles):
            if c == N1:
                x_copy(t).wait()
            at = slice(t * TILE, (t + 1) * TILE)
            z = dot(pick, y_ref[:, at]).astype(BF16)
            if c == L:
                zr[0:slots, at] = z[0:slots]
                zs[0:slots, at] = z[slots:pair]
            else:
                zs[sent(c), at] = z

    dispatch(N1)
    dispatch(L)
    pl.semaphore_wait(barrier, len(BLOCKS) - 1)
    z_copy(2 * N1).start()
    z_copy(2 * N1 + 1).start()
    z_copy(2 * L + 1).start()
    dispatch(O)
    z_copy(2 * O).start()
    z_copy(2 * O + 1).start()
    fresh = units - RING

    def project(at, unit, first, count, into):
        z = zr[first:first + count, :]
        a = dot(z, w1[at, 0])
        b = dot(z, w1[at, 1])
        h[into:into + count, columns(unit, UNIT)] = (a * jax.nn.sigmoid(a) * b).astype(BF16)

    def up_pass(turn, c):
        def place(p):
            return lax.rem(units * turn + p, RING)

        def unit_of(p):
            return lax.rem(p + fresh * turn, units)

        def step(i, _):
            for p in (2 * i, 2 * i + 1):
                pl.when(p >= RING)(functools.partial(w1_wait, place(p)))
            for p in (2 * i, 2 * i + 1):
                project(place(p), unit_of(p), c * pair, pair, pair)

            @pl.when(i < fresh // 2)
            def _():
                for p in (2 * i, 2 * i + 1):
                    w1_start(unit_of(p + RING), place(p))

            return 0

        lax.fori_loop(0, units // 2, step, 0)
        w1_wait(place(units - 1))
        project(place(units - 1), unit_of(units - 1), c * pair, pair, pair)

    def first_own(p, _):
        w1_wait(p)
        project(p, p, 0, pair, 0)
        return 0

    def first_near(i, _):
        for p in (2 * i, 2 * i + 1):
            project(p, p, pair, pair, pair)

        @pl.when(i < fresh // 2)
        def _():
            for p in (2 * i, 2 * i + 1):
                w1_start(p + RING, p)

        return 0

    def first_both(p, _):
        w1_wait(p)
        for c in (L, N1):
            project(p, p + RING, c * pair, pair, c * pair)

        @pl.when(p == SEND_N2)
        def _():
            z_copy(2 * N2).start()
            z_copy(2 * N2 + 1).start()

        return 0

    def down_pass(c, first=False):
        for block in (2 * c, 2 * c + 1):
            if block:
                z_copy(block).wait_send()

        for start in range(0, tiles, BATCH):
            batch = range(start, start + BATCH)
            for tile in batch:
                if first:
                    w2_copy(tile).wait()
            for tile in batch:
                out = dot(h[hidden(c), :], w2[tile]).astype(BF16)
                if c == L:
                    orv[tile, 0:slots, :] = out[0:slots]
                    zs[0:slots, columns(tile, TILE)] = out[slots:pair]
                else:
                    zs[sent(c), columns(tile, TILE)] = out
            for tile in batch:
                if c != L:
                    o_copy(tile, 2 * c).start()
                o_copy(tile, 2 * c + 1).start()

    def wait_z(c):
        z_arrived(2 * c)
        z_arrived(2 * c + 1)

    for tile in range(tiles):
        w2_copy(tile).start(priority=1)
    z_arrived(2 * L + 1)
    lax.fori_loop(0, RING, first_own, 0)
    dispatch(N2)

    wait_z(N1)
    lax.fori_loop(0, RING // 2, first_near, 0)
    project(RING - 1, RING - 1, pair, pair, pair)
    lax.fori_loop(0, fresh, first_both, 0)
    down_pass(N1, first=True)
    def weighs(c, part):
        half = tokens // 2
        at = (2 * c + part) * half * 2
        return slice(pair, pair + half), slice(at, at + pair)

    table = jnp.concatenate([code.astype(F32), gate[...], jnp.zeros((124, tokens), F32)], axis=0).T
    for c in range(4):
        column = bases(lax.broadcasted_iota(jnp.int32, (tokens, pair), 1), c).astype(F32)
        weight = jnp.where(table[:, 0:1] == column, table[:, 2:3], 0.0)
        weight = weight + jnp.where(table[:, 1:2] == column, table[:, 3:4], 0.0)
        weight = weight.astype(BF16)
        for part in range(2):
            zr[weighs(c, part)] = weight[part * (tokens // 2):(part + 1) * (tokens // 2)]

    wait_z(O)
    up_pass(1, O)
    down_pass(O)
    wait_z(N2)
    up_pass(2, N2)
    down_pass(N2)
    down_pass(L)

    for tile in range(tiles):
        for block in range(1, len(BLOCKS)):
            o_arrived(tile, block)
        for part in range(2):
            total = dot(zr[weighs(0, part)], orv[tile, chunk(0), :])
            for c in range(1, 4):
                total = total + dot(zr[weighs(c, part)], orv[tile, chunk(c), :])
            half = tokens // 2
            y_ref[part * half:(part + 1) * half, tile * TILE:(tile + 1) * TILE] = total.astype(BF16)

    for block in range(1, len(BLOCKS)):
        for tile in range(tiles):
            o_copy(tile, block).wait_send()


SEND_N2 = 1
BATCH = 2


def solution(mesh):
    def body(x, expert, slot, gate, w_gate, w_up, w_down):
        tokens, d = x.shape[2:]
        top = expert.shape[3]
        held, _, ff = w_gate.shape
        experts = held * mesh.shape["ep"]
        slots = 5 * tokens * top // (4 * experts)
        rows = experts * slots
        vmem = pl.BlockSpec(memory_space=pltpu.VMEM)
        hbm = pl.BlockSpec(memory_space=pltpu.HBM)
        tiles = d // TILE
        dma = pltpu.SemaphoreType.DMA
        y = pl.pallas_call(
            functools.partial(kernel, slots),
            name="moe",
            out_shape=OUT((tokens, d), BF16),
            in_specs=[vmem, vmem, vmem, hbm, hbm, hbm, hbm],
            out_specs=vmem,
            scratch_shapes=[
                pltpu.VMEM((rows - slots, d), BF16),
                pltpu.VMEM((rows, d), BF16),
                pltpu.VMEM((4 * slots, ff), BF16),
                pltpu.VMEM((tiles, rows, TILE), BF16),
                pltpu.VMEM((RING, 2, d, UNIT), BF16),
                pltpu.VMEM((tiles, ff, TILE), BF16),
                dma((tiles,)),
                dma((RING, 2)),
                dma((tiles,)),
                dma((8,)),
                dma((8,)),
                dma((tiles, 8)),
                dma((tiles, 8)),
            ],
            compiler_params=pltpu.CompilerParams(
                collective_id=0, has_side_effects=True, vmem_limit_bytes=LIMIT
            ),
        )(expert[0, 0].T, slot[0, 0].T, gate[0, 0].T, x[0, 0], w_gate, w_up, w_down)
        return y[None, None]

    part = P("dp", "ep")
    weights = P("ep")
    return jax.shard_map(
        body, mesh=mesh, in_specs=(part, part, part, part, weights, weights, weights), out_specs=part, check_vma=False
    )


OUT = pltpu.VMEM
LIMIT = 65_800_000
```

time: 75.3 us -> 67.5 us (0.90)
  Pallas kernels: 74.1 us -> 66.4 us
    pallas_call x1, Pallas kernels: 74.1 us -> 66.4 us  [body(): pl.pallas_call(functools.partial(kernel, slots), name='moe', out_shape=OU...]
where the time goes in v3:
time: 67.5 us; the launch traced here: 67.4 us
  Pallas kernels  66.4 us (98%)
  local copies, waits for them, and re-layouts  0.97 us (1%)
    pallas_call x1, Pallas kernels, body(): pl.pallas_call(functools.partial(kernel, slots), name='moe', out_shape=OU...  66.4 us

profile of v3, /device:TPU:113, one launch (start us, length us, event | category | flops | bytes accessed | tf_op | source)
XLA Modules:
  0.0 67.4 jit_solution(12967856332082238194)
XLA Ops:
  0.0 66.4 %moe.1 = bf16[256,2048]{1,0:T(8,128)(2,1)S(1)} custom-call(s32[2,256]{1,0:T(2,128)} %bitcast.13, s32[2,256]{1,0:T(2,128)} %bitcast.14, f32[2,256]{1,0:T(2,128)} %bitcast.15, bf16[256,2048]{1,0:T(8,128)(2,1)} %bitcast.12, bf16[2,2048,5632]{2,1,0:T(8,128)(2,1)} %wg.1, bf16[2,2048,5632]{2,1,0:T(8,128)(2,1)} %wu.1, bf16[2,5632,2048]{2,1,0:T(8,128)(2,1)} %wd.1), custom_call_target="tpu_custom_call" | custom-call | tf_op jit(solution)/shard_map/moe/pallas_call | solution.py:293
  66.5 1.0 %copy.9 = bf16[1,1,256,2048]{3,2,1,0:T(8,128)(2,1)} copy(bf16[1,1,256,2048]{3,2,1,0:T(8,128)(2,1)S(1)} %bitcast.11) | data formatting | bytes 2097152

commit v4 on v3

--- a/solution.py
+++ b/solution.py
@@ -132,12 +132,12 @@
                 zs[sent(c), at] = z
 
     dispatch(N1)
-    dispatch(L)
     pl.semaphore_wait(barrier, len(BLOCKS) - 1)
     z_copy(2 * N1).start()
     z_copy(2 * N1 + 1).start()
+    dispatch(L)
+    dispatch(O)
     z_copy(2 * L + 1).start()
-    dispatch(O)
     z_copy(2 * O).start()
     z_copy(2 * O + 1).start()
     fresh = units - RING
@@ -275,7 +275,7 @@
 
 
 SEND_N2 = 1
-BATCH = 2
+BATCH = 1
 
 
 def solution(mesh):

time: 67.5 us -> 67 us (level)
  no operation moved by 1% of the time
where the time goes in v4:
time: 67 us; the launch traced here: 66.8 us
  Pallas kernels  65.9 us (98%)
  local copies, waits for them, and re-layouts  0.97 us (1%)
    pallas_call x1, Pallas kernels, body(): pl.pallas_call(functools.partial(kernel, slots), name='moe', out_shape=OU...  65.9 us

profile of v4, /device:TPU:113, one launch (start us, length us, event | category | flops | bytes accessed | tf_op | source)
XLA Modules:
  0.0 66.8 jit_solution(200972902816459148)
XLA Ops:
  0.0 65.9 %moe.1 = bf16[256,2048]{1,0:T(8,128)(2,1)S(1)} custom-call(s32[2,256]{1,0:T(2,128)} %bitcast.13, s32[2,256]{1,0:T(2,128)} %bitcast.14, f32[2,256]{1,0:T(2,128)} %bitcast.15, bf16[256,2048]{1,0:T(8,128)(2,1)} %bitcast.12, bf16[2,2048,5632]{2,1,0:T(8,128)(2,1)} %wg.1, bf16[2,2048,5632]{2,1,0:T(8,128)(2,1)} %wu.1, bf16[2,5632,2048]{2,1,0:T(8,128)(2,1)} %wd.1), custom_call_target="tpu_custom_call" | custom-call | tf_op jit(solution)/shard_map/moe/pallas_call | solution.py:293
  65.9 1.0 %copy.9 = bf16[1,1,256,2048]{3,2,1,0:T(8,128)(2,1)} copy(bf16[1,1,256,2048]{3,2,1,0:T(8,128)(2,1)S(1)} %bitcast.11) | data formatting | bytes 2097152

commit v5 on v4

--- a/solution.py
+++ b/solution.py
@@ -260,12 +260,18 @@
     down_pass(L)
 
     for tile in range(tiles):
-        for block in range(1, len(BLOCKS)):
+        for block in range(1, 2 * N2):
+            o_arrived(tile, block)
+        totals = []
+        for part in range(2):
+            total = dot(zr[weighs(0, part)], orv[tile, chunk(0), :])
+            for c in range(1, N2):
+                total = total + dot(zr[weighs(c, part)], orv[tile, chunk(c), :])
+            totals.append(total)
+        for block in (2 * N2, 2 * N2 + 1):
             o_arrived(tile, block)
         for part in range(2):
-            total = dot(zr[weighs(0, part)], orv[tile, chunk(0), :])
-            for c in range(1, 4):
-                total = total + dot(zr[weighs(c, part)], orv[tile, chunk(c), :])
+            total = totals[part] + dot(zr[weighs(N2, part)], orv[tile, chunk(N2), :])
             half = tokens // 2
             y_ref[part * half:(part + 1) * half, tile * TILE:(tile + 1) * TILE] = total.astype(BF16)
 

time: 67 us -> 66.7 us (level)
  no operation moved by 1% of the time
where the time goes in v5:
time: 66.7 us; the launch traced here: 66.6 us
  Pallas kernels  65.7 us (99%)
  local copies, waits for them, and re-layouts  0.97 us (1%)
    pallas_call x1, Pallas kernels, body(): pl.pallas_call(functools.partial(kernel, slots), name='moe', out_shape=OU...  65.7 us

profile of v5, /device:TPU:113, one launch (start us, length us, event | category | flops | bytes accessed | tf_op | source)
XLA Modules:
  0.0 66.6 jit_solution(11728517500453273315)
XLA Ops:
  0.0 65.7 %moe.1 = bf16[256,2048]{1,0:T(8,128)(2,1)S(1)} custom-call(s32[2,256]{1,0:T(2,128)} %bitcast.13, s32[2,256]{1,0:T(2,128)} %bitcast.14, f32[2,256]{1,0:T(2,128)} %bitcast.15, bf16[256,2048]{1,0:T(8,128)(2,1)} %bitcast.12, bf16[2,2048,5632]{2,1,0:T(8,128)(2,1)} %wg.1, bf16[2,2048,5632]{2,1,0:T(8,128)(2,1)} %wu.1, bf16[2,5632,2048]{2,1,0:T(8,128)(2,1)} %wd.1), custom_call_target="tpu_custom_call" | custom-call | tf_op jit(solution)/shard_map/moe/pallas_call | solution.py:299
  65.7 1.0 %copy.9 = bf16[1,1,256,2048]{3,2,1,0:T(8,128)(2,1)} copy(bf16[1,1,256,2048]{3,2,1,0:T(8,128)(2,1)S(1)} %bitcast.11) | data formatting | bytes 2097152
